TPU v7x, 32 devices: a whole 2x2x4 slice. The times are simulated.
32 devices in a mesh: row: 4 (over y, core), col: 4 (over z), layer: 2 (over x).
Axes of the slice: x: 2, y: 2, z: 4, core: 2. Of those that a mesh axis runs over, the one named last changes fastest.
Arguments:
- a_tiles: float32 [16, 2, 7, 128, 128], P(('row', 'col'), 'layer'), may hold values from -0.5 to 0.5
- a_cols: int32 [16, 2, 7], P(('row', 'col'), 'layer'), may hold values from -1 to 255, as said below
- b_tiles: float32 [256, 2, 7, 128, 128], P(('row', 'col'), 'layer'), may hold values from -6 to 6
- b_rows: int32 [256, 2, 7], P(('row', 'col'), 'layer'), may hold values from 0 to 255, as said below
- c_cols: int32 [16, 4, 4], P('row', 'col'), may hold values from 0 to 255, as said below
Outputs:
- c_tiles: float32 [16, 4, 4, 128, 128], P('row', 'col', 'layer')
Inputs may be any that keep to these rules, and one draw needn't show every extreme that they name: In a_cols[i, h, :] the used slots come first and hold distinct block columns in [h * 128, (h + 1) * 128); the unused ones hold -1. Some block rows use all 7 slots in each half, others few. b_rows[j, h, :] holds 7 distinct block rows in [h * 128, (h + 1) * 128). c_cols[i, g, :] holds 4 distinct block columns j with (j // 16) % 4 == g.
All inputs are finite; a program needn't handle non-finite values.
Results may differ from a plain program's by a relative error of at most 0.0003.
Values sent between devices are 32-bit elements; how exact they have to be, the bound alone decides.
No kernel may reach another device: no remote copies, remote signals or barrier semaphores. Data moves between devices by JAX's collectives and lax.ppermute only.
A program may use at most 128 MiB of HBM per device.

v0:
```python
import jax
import jax.numpy as jnp
from jax import lax
from jax.sharding import PartitionSpec as P


def row_block(a_row, a_index, wanted, b_flat, b_index, block_width, group_count):
    halves = b_index.shape[1]
    slot_count = b_index.shape[2]
    panel_col = wanted // block_width // group_count * block_width + wanted % block_width
    col_rows = b_index[panel_col]
    matches = (col_rows[:, :, None, :] == a_index[None, :, :, None]) & (a_index >= 0)[
        None, :, :, None
    ]
    present = jnp.any(matches, axis=3)
    position = jnp.argmax(matches, axis=3)
    layer_ids = jnp.arange(halves, dtype=jnp.int32)
    flat_index = (
        panel_col[:, None, None] * halves + layer_ids[None, :, None]
    ) * slot_count + position
    chosen = jnp.take(b_flat, flat_index.reshape(-1), axis=0)
    chosen = chosen.reshape(flat_index.shape + b_flat.shape[1:])
    chosen = jnp.where(present[..., None, None], chosen, jnp.zeros((), chosen.dtype))
    return jnp.einsum("heab,qhebc->qac", a_row, chosen, precision=lax.Precision.HIGHEST)


def on_device(a_tiles, a_cols, b_tiles, b_rows, c_cols):
    block_width = b_tiles.shape[0]
    group_count = lax.axis_size("col")
    wanted = c_cols[:, 0, :]
    b_panel, b_index = (
        lax.all_gather(b_tiles, "row", axis=0, tiled=True),
        lax.all_gather(b_rows, "row", axis=0, tiled=True),
    )
    b_flat = b_panel.reshape((-1,) + b_panel.shape[3:])
    a_piece = lax.all_gather(a_tiles, "col", axis=0, tiled=True)
    index_piece = lax.all_gather(a_cols, "col", axis=0, tiled=True)

    def one_row(inputs):
        return row_block(inputs[0], inputs[1], inputs[2], b_flat, b_index, block_width, group_count)

    row_out = lax.map(one_row, (a_piece, index_piece, wanted))
    return lax.psum_scatter(row_out[:, None], "layer", scatter_dimension=2, tiled=True)


def solution(mesh):
    return jax.shard_map(
        on_device,
        mesh=mesh,
        in_specs=(
            P(("row", "col"), "layer", None, None, None),
            P(("row", "col"), "layer", None),
            P(("row", "col"), "layer", None, None, None),
            P(("row", "col"), "layer", None),
            P("row", "col", None),
        ),
        out_specs=P("row", "col", "layer", None, None),
        check_vma=False,
    )
```

profile of v0, /device:TPU:0, one launch (start us, length us, event | category | flops | bytes accessed | tf_op | source)
XLA Modules:
  0.0 355.9 jit_solution(14244354219094431181)
XLA Ops:
  6.5 0.0 all-gather.5.cloned.1.call-start
  6.5 0.7 all-gather.5.cloned.1.call-update
  7.3 0.0 copy-start.1
  7.3 0.0 copy-start
  7.3 0.0 copy-start.2
  7.3 0.0 all-gather.3.cloned.1.call-start
  7.3 0.7 all-gather.3.cloned.1.call-update
  8.0 0.0 all-reduce.3.cloned.1.call-start
  8.1 0.0 copy-done.1
  8.1 12.6 %all_gather.13 = s32[4,1,7]{2,1,0:T(1,128)S(1)} all-gather(s32[1,1,7]{2,1,0:T(1,128)S(1)} %copy-done.1), channel_id=1, replica_groups=mesh['row'=4,'col'=4,'layer'=2] {'col'}, dimensions={0}, use_global_device_ids=true | all-gather | bytes 140 | tf_op jit(solution)/shard_map/all_gather | solution.py:37
  20.7 0.1 copy.18
  20.8 5.2 %all_gather.12 = s32[64,1,7]{2,0,1:T(8,128)S(1)} all-gather(s32[16,1,7]{2,0,1:T(8,128)S(1)} %copy.18), channel_id=1, replica_groups=mesh['row'=4,'col'=4,'layer'=2] {'row'}, dimensions={0}, use_global_device_ids=true | all-gather | bytes 2240 | tf_op jit(solution)/shard_map/all_gather | solution.py:33
  26.0 27.0 %all-gather.5.cloned.1.call-done = f32[4,1,7,128,128]{4,3,2,1,0:T(8,128)} async-done(((f32[1,1,7,128,128]{4,3,2,1,0:T(8,128)}), f32[4,1,7,128,128]{4,3,2,1,0:T(8,128)}) %all-gather.5.cloned.1.call-update) | async-done | bytes 1835024 | tf_op jit(solution)/shard_map/all_gather | solution.py:36
  53.0 178.4 %all-gather.3.cloned.1.call-done = f32[64,1,7,128,128]{4,3,2,1,0:T(8,128)} async-done(((f32[16,1,7,128,128]{4,3,2,1,0:T(8,128)}), f32[64,1,7,128,128]{4,3,2,1,0:T(8,128)}) %all-gather.3.cloned.1.call-update) | async-done | bytes 29360144 | tf_op jit(solution)/shard_map/all_gather | solution.py:32
  231.4 75.8 %while.13 = (s32[]{:T(128)}, f32[4,4,128,128]{3,2,1,0:T(8,128)}, s32[4,4]{1,0:T(4,128)S(1)}, s32[64,1,7]{2,0,1:T(8,128)S(1)}, s32[4,1,7]{2,1,0:T(1,128)S(1)}, /*...) while((s32[]{:T(128)}, f32[4,4,128,128]{3,2,1,0:T(8,128)}, s32[4,4]{1,0:T(4,128)S(1)}, ...), condition=%wide.region_3.4_spmd, body=%wide.region_0.3_spmd.sunk | while | flops 705565312 | bytes 10955050 | solution.py:42
  231.5 0.6 gather_fusion
  232.1 0.3 fusion.35
  232.3 0.1 copy.31
  232.4 1.0 iota_reduce_fusion.2
  233.4 0.1 copy.29
  233.5 0.1 reshape.402
  233.6 11.3 %gather_fusion.1 = f32[28,128,128]{2,1,0:T(8,128)} fusion(f32[448,128,128]{2,1,0:T(8,128)} %get-tuple-element.214, s32[1024]{0:T(1024)S(1)} %pad_clamp_fusion.5), kind=kCustom, calls=%fused_computation.1.clone.1 | custom fusion | bytes 3670128 | tf_op jit(solution)/shard_map/while/body/eval_jaxpr/jit(_take)/gather | solution.py:21
  244.9 1.8 copy.30
  246.7 2.8 fusion.36
  249.5 0.1 copy.32
  249.6 0.7 constant_dynamic-update-slice_fusion.2
  250.4 0.6 gather_fusion
  251.0 0.3 fusion.35
  251.3 0.1 copy.31
  251.4 1.0 iota_reduce_fusion.2
  252.4 0.1 copy.29
  252.5 0.1 reshape.402
  252.6 11.3 %gather_fusion.1 = f32[28,128,128]{2,1,0:T(8,128)} fusion(f32[448,128,128]{2,1,0:T(8,128)} %get-tuple-element.214, s32[1024]{0:T(1024)S(1)} %pad_clamp_fusion.5), kind=kCustom, calls=%fused_computation.1.clone.1 | custom fusion | bytes 3670128 | tf_op jit(solution)/shard_map/while/body/eval_jaxpr/jit(_take)/gather | solution.py:21
  263.8 1.8 copy.30
  265.7 2.8 fusion.36
  268.4 0.1 copy.32
  268.6 0.7 constant_dynamic-update-slice_fusion.2
  269.4 0.6 gather_fusion
  270.0 0.3 fusion.35
  270.2 0.1 copy.31
  270.3 1.0 iota_reduce_fusion.2
  271.3 0.1 copy.29
  271.4 0.1 reshape.402
  271.5 11.3 %gather_fusion.1 = f32[28,128,128]{2,1,0:T(8,128)} fusion(f32[448,128,128]{2,1,0:T(8,128)} %get-tuple-element.214, s32[1024]{0:T(1024)S(1)} %pad_clamp_fusion.5), kind=kCustom, calls=%fused_computation.1.clone.1 | custom fusion | bytes 3670128 | tf_op jit(solution)/shard_map/while/body/eval_jaxpr/jit(_take)/gather | solution.py:21
  282.8 1.8 copy.30
  284.6 2.8 fusion.36
  287.4 0.1 copy.32
  287.5 0.7 constant_dynamic-update-slice_fusion.2
  288.3 0.6 gather_fusion
  288.9 0.3 fusion.35
  289.2 0.1 copy.31
  289.3 1.0 iota_reduce_fusion.2
  290.3 0.1 copy.29
  290.4 0.1 reshape.402
  290.5 11.3 %gather_fusion.1 = f32[28,128,128]{2,1,0:T(8,128)} fusion(f32[448,128,128]{2,1,0:T(8,128)} %get-tuple-element.214, s32[1024]{0:T(1024)S(1)} %pad_clamp_fusion.5), kind=kCustom, calls=%fused_computation.1.clone.1 | custom fusion | bytes 3670128 | tf_op jit(solution)/shard_map/while/body/eval_jaxpr/jit(_take)/gather | solution.py:21
  301.7 1.8 copy.30
  303.6 2.8 fusion.36
  306.3 0.1 copy.32
  306.5 0.7 constant_dynamic-update-slice_fusion.2
  307.2 0.0 all-reduce.3.cloned.1.call-update
  307.2 0.0 copy-done.3
  307.2 0.6 dynamic-slice
  308.5 39.0 %all-reduce.3.cloned.1.call-done = f32[4,1,4,128,128]{4,3,2,1,0:T(8,128)} async-done(((f32[4,1,4,128,128]{4,3,2,1,0:T(8,128)}), f32[4,1,4,128,128]{4,3,2,1,0:T(8,128)}) %all-reduce.3.cloned.1.call-update) | async-done | bytes 1048592
  347.5 1.9 constant_dynamic-slice_fusion.2
  (36 shorter events, 0.4 us)
Async XLA Ops:
  6.5 46.5 %all-gather.5.cloned.1.call-start = ((), (), s32[]{:S(2)}) async-start(), calls=%async_computation.1 | async-start | bytes 2293760 | tf_op jit(solution)/shard_map/all_gather | solution.py:36
  7.3 0.8 copy-start.1
  7.3 13.5 %copy-start = (s32[16,1,7]{0,1,2:T(1,128)S(1)}, s32[16,1,7]{0,1,2:T(1,128)}, u32[]{:S(2)}) copy-start(s32[16,1,7]{0,1,2:T(1,128)} %param.10) | copy-start | bytes 1348
  7.3 224.1 %copy-start.2 = (s32[4,1,4]{2,1,0:T(1,128)S(1)}, s32[4,1,4]{2,1,0:T(1,128)}, u32[]{:S(2)}) copy-start(s32[4,1,4]{2,1,0:T(1,128)} %param.11) | copy-start | bytes 196
  7.3 224.1 %all-gather.3.cloned.1.call-start = ((), (), s32[]{:S(2)}) async-start(), calls=%async_computation | async-start | bytes 36700160 | tf_op jit(solution)/shard_map/all_gather | solution.py:32
  8.0 339.4 %all-reduce.3.cloned.1.call-start = ((), (), s32[]{:S(2)}) async-start(), calls=%async_computation.2 | async-start | bytes 2097152
  231.4 75.8 %copy-start.3 = (u32[32]{0:T(128)S(1)}, u32[32]{0:T(128)}, u32[]{:S(2)}) copy-start(u32[32]{0:T(128)} %constant.166) | copy-start | bytes 388
Sparse Core Ops, SparseCore 0:
  8.9 44.0 all-gather.4
  54.6 176.7 all-gather.2
  307.3 40.0 all-reduce.2
where the time goes:
time: 356 us
  waiting for transfers between devices  246 us (69%)
  local copies, waits for them, and re-layouts  61.7 us (17%)
  blocking collectives  17.8 us (5%)
  between operations  13.8 us (4%)
  matrix products  11.1 us (3%)
  other arithmetic  5.41 us (2%)
    all_gather x1, waiting for transfers between devices, on_device(): lax.all_gather(b_tiles, 'row', axis=0, tiled=True)  178 us
    gather x8, local copies, waits for them, and re-layouts, row_block(): chosen = jnp.take(b_flat, flat_index.reshape(-1), axis=0)  52.3 us
    unnamed x4, waiting for transfers between devices  40.4 us
    all_gather x1, waiting for transfers between devices, on_device(): a_piece = lax.all_gather(a_tiles, 'col', axis=0, tiled=True)  27 us
    all_gather x1, blocking collectives, on_device(): index_piece = lax.all_gather(a_cols, 'col', axis=0, tiled=True)  12.6 us
    dot_general x4, matrix products, row_block(): jnp.einsum('heab,qhebc->qac', a_row, chosen, precision=lax.Precision.HIGH...  11.1 us
  transfers between devices with their start and end apart: 3, of which 3 were waited for; matrix products, arithmetic and copies ran while one was open for 0% of the time, Pallas kernels for 0%

commit v1 on v0

--- a/solution.py
+++ b/solution.py
@@ -33,7 +33,14 @@
         lax.all_gather(b_rows, "row", axis=0, tiled=True),
     )
     b_flat = b_panel.reshape((-1,) + b_panel.shape[3:])
-    a_piece = lax.all_gather(a_tiles, "col", axis=0, tiled=True)
+    size = lax.axis_size("col")
+    route = [(i, (i + 1) % size) for i in range(size)]
+    parts = [a_tiles]
+    for stride in range(1, size):
+        parts = [lax.ppermute(parts[0], "col", route), *parts]
+    whole = jnp.concatenate(parts, axis=0)
+    shift = (lax.axis_index("col") + 1) * parts[-1].shape[0]
+    a_piece = jnp.roll(whole, shift, axis=0)
     index_piece = lax.all_gather(a_cols, "col", axis=0, tiled=True)
 
     def one_row(inputs):

time: 356 us -> 315 us (0.88)
  waiting for transfers between devices: 246 us -> 197 us
    all_gather x1, waiting for transfers between devices: 178 us -> 131 us  [on_device(): lax.all_gather(b_tiles, 'row', axis=0, tiled=True)]
    all_gather x1 -> x0, waiting for transfers between devices: 27 us -> none  [on_device(): a_piece = lax.all_gather(a_tiles, 'col', axis=0, tiled=True)]
    ppermute x0 -> x3, waiting for transfers between devices: none -> 26 us  [on_device(): parts = [lax.ppermute(parts[0], 'col', route), *parts]]
    unnamed x4 -> x3, waiting for transfers between devices: 40.4 us -> 39.7 us
  transfers between devices with their start and end apart: 3 -> 5, of which waited for: 3 -> 4; matrix products, arithmetic and copies ran while one was open for 0% -> 1% of each run, Pallas kernels for 0% -> 0%
where the time goes in v1:
time: 315 us
  waiting for transfers between devices  197 us (63%)
  local copies, waits for them, and re-layouts  63.6 us (20%)
  blocking collectives  19.9 us (6%)
  between operations  14.1 us (4%)
  matrix products  11.3 us (4%)
  other arithmetic  5.38 us (2%)
    all_gather x1, waiting for transfers between devices, on_device(): lax.all_gather(b_tiles, 'row', axis=0, tiled=True)  131 us
    gather x8, local copies, waits for them, and re-layouts, row_block(): chosen = jnp.take(b_flat, flat_index.reshape(-1), axis=0)  52.3 us
    unnamed x3, waiting for transfers between devices  39.7 us
    ppermute x3, waiting for transfers between devices, on_device(): parts = [lax.ppermute(parts[0], 'col', route), *parts]  26 us
    all_gather x1, blocking collectives, on_device(): index_piece = lax.all_gather(a_cols, 'col', axis=0, tiled=True)  14.5 us
    dot_general x4, matrix products, row_block(): jnp.einsum('heab,qhebc->qac', a_row, chosen, precision=lax.Precision.HIGH...  11.3 us
  transfers between devices with their start and end apart: 5, of which 4 were waited for; matrix products, arithmetic and copies ran while one was open for 1% of the time, Pallas kernels for 0%

profile of v1, /device:TPU:0, one launch (start us, length us, event | category | flops | bytes accessed | tf_op | source)
XLA Modules:
  0.0 314.8 jit_solution(1192702088288874146)
XLA Ops:
  6.5 0.7 all-gather.2.cloned.1.call-update
  7.3 0.0 all-reduce.3.cloned.1.call-start
  7.3 0.2 copy-done
  7.6 3.1 collective-permute-start
  10.6 12.5 %collective-permute-done = f32[1,1,7,128,128]{4,3,2,1,0:T(8,128)S(1)} collective-permute-done((f32[1,1,7,128,128]{4,3,2,1,0:T(8,128)S(1)}, f32[1,1,7,128,128]{4,3,2,1,0:T(8,128)S(1)}, u32[]{:S(2)}, u32[]{:S(2)}) %collective-permute-start) | collective-permute-done | bytes 458784 | tf_op jit(solution)/shard_map/ppermute | solution.py:40
  23.1 0.0 collective-permute-start.1
  23.2 13.5 %collective-permute-done.1 = f32[1,1,7,128,128]{4,3,2,1,0:T(8,128)S(1)} collective-permute-done((f32[1,1,7,128,128]{4,3,2,1,0:T(8,128)S(1)}, f32[1,1,7,128,128]{4,3,2,1,0:T(8,128)S(1)}, u32[]{:S(2)}, u32[]{:S(2)}) %collective-permute-start.1) | collective-permute-done | bytes 458784 | tf_op jit(solution)/shard_map/ppermute | solution.py:40
  36.6 0.0 collective-permute-start.2
  36.6 14.5 %all_gather.10 = s32[4,1,7]{2,1,0:T(1,128)S(1)} all-gather(s32[1,1,7]{2,1,0:T(1,128)S(1)} %copy-done.2), channel_id=1, replica_groups=mesh['row'=4,'col'=4,'layer'=2] {'col'}, dimensions={0}, use_global_device_ids=true | all-gather | bytes 140 | tf_op jit(solution)/shard_map/all_gather | solution.py:44
  51.1 0.1 copy.18
  51.2 5.5 %all_gather.9 = s32[64,1,7]{2,0,1:T(8,128)S(1)} all-gather(s32[16,1,7]{2,0,1:T(8,128)S(1)} %copy.18), channel_id=1, replica_groups=mesh['row'=4,'col'=4,'layer'=2] {'row'}, dimensions={0}, use_global_device_ids=true | all-gather | bytes 2240 | tf_op jit(solution)/shard_map/all_gather | solution.py:33
  56.7 0.0 collective-permute-done.2
  56.8 0.0 copy-start.3
  57.0 1.5 constant_dynamic-slice_fusion.3
  58.5 131.4 %all-gather.2.cloned.1.call-done = f32[64,1,7,128,128]{4,3,2,1,0:T(8,128)} async-done(((f32[16,1,7,128,128]{4,3,2,1,0:T(8,128)}), f32[64,1,7,128,128]{4,3,2,1,0:T(8,128)}) %all-gather.2.cloned.1.call-update) | async-done | bytes 29360144 | tf_op jit(solution)/shard_map/all_gather | solution.py:32
  189.8 76.0 %while.13 = (s32[]{:T(128)}, f32[4,4,128,128]{3,2,1,0:T(8,128)}, s32[4,4]{1,0:T(4,128)S(1)}, s32[64,1,7]{2,0,1:T(8,128)S(1)}, s32[4,1,7]{2,1,0:T(1,128)S(1)}, /*...) while((s32[]{:T(128)}, f32[4,4,128,128]{3,2,1,0:T(8,128)}, s32[4,4]{1,0:T(4,128)S(1)}, ...), condition=%wide.region_3.4_spmd, body=%wide.region_0.3_spmd.sunk | while | flops 705565312 | bytes 10956058 | solution.py:49
  189.9 0.6 gather_fusion
  190.4 1.0 iota_reduce_fusion.2
  191.4 0.1 copy.29
  191.5 0.1 reshape.402
  191.6 11.3 %gather_fusion.1 = f32[28,128,128]{2,1,0:T(8,128)} fusion(f32[448,128,128]{2,1,0:T(8,128)} %get-tuple-element.214, s32[1024]{0:T(1024)S(1)} %pad_clamp_fusion.5), kind=kCustom, calls=%fused_computation.1.clone.1 | custom fusion | bytes 3670128 | tf_op jit(solution)/shard_map/while/body/eval_jaxpr/jit(_take)/gather | solution.py:21
  202.9 1.8 copy.30
  204.7 0.3 fusion.35
  205.0 0.1 copy.31
  205.1 2.8 fusion.36
  208.0 0.1 copy.32
  208.1 0.7 constant_dynamic-update-slice_fusion.10
  208.9 0.6 gather_fusion
  209.4 1.0 iota_reduce_fusion.2
  210.4 0.1 copy.29
  210.5 0.1 reshape.402
  210.6 11.3 %gather_fusion.1 = f32[28,128,128]{2,1,0:T(8,128)} fusion(f32[448,128,128]{2,1,0:T(8,128)} %get-tuple-element.214, s32[1024]{0:T(1024)S(1)} %pad_clamp_fusion.5), kind=kCustom, calls=%fused_computation.1.clone.1 | custom fusion | bytes 3670128 | tf_op jit(solution)/shard_map/while/body/eval_jaxpr/jit(_take)/gather | solution.py:21
  221.9 1.8 copy.30
  223.7 0.3 fusion.35
  224.0 0.1 copy.31
  224.1 2.8 fusion.36
  227.0 0.1 copy.32
  227.1 0.7 constant_dynamic-update-slice_fusion.10
  227.9 0.6 gather_fusion
  228.5 1.0 iota_reduce_fusion.2
  229.4 0.1 copy.29
  229.5 0.1 reshape.402
  229.6 11.3 %gather_fusion.1 = f32[28,128,128]{2,1,0:T(8,128)} fusion(f32[448,128,128]{2,1,0:T(8,128)} %get-tuple-element.214, s32[1024]{0:T(1024)S(1)} %pad_clamp_fusion.5), kind=kCustom, calls=%fused_computation.1.clone.1 | custom fusion | bytes 3670128 | tf_op jit(solution)/shard_map/while/body/eval_jaxpr/jit(_take)/gather | solution.py:21
  240.9 1.8 copy.30
  242.7 0.3 fusion.35
  243.0 0.1 copy.31
  243.1 2.8 fusion.36
  246.0 0.1 copy.32
  246.1 0.7 constant_dynamic-update-slice_fusion.10
  246.9 0.6 gather_fusion
  247.4 1.0 iota_reduce_fusion.2
  248.4 0.1 copy.29
  248.5 0.1 reshape.402
  248.6 11.3 %gather_fusion.1 = f32[28,128,128]{2,1,0:T(8,128)} fusion(f32[448,128,128]{2,1,0:T(8,128)} %get-tuple-element.214, s32[1024]{0:T(1024)S(1)} %pad_clamp_fusion.5), kind=kCustom, calls=%fused_computation.1.clone.1 | custom fusion | bytes 3670128 | tf_op jit(solution)/shard_map/while/body/eval_jaxpr/jit(_take)/gather | solution.py:21
  259.9 1.8 copy.30
  261.7 0.3 fusion.35
  262.0 0.1 copy.31
  262.1 2.8 fusion.36
  265.0 0.1 copy.32
  265.1 0.7 constant_dynamic-update-slice_fusion.10
  265.8 0.0 all-reduce.3.cloned.1.call-update
  265.9 0.6 dynamic-slice
  267.1 39.0 %all-reduce.3.cloned.1.call-done = f32[4,1,4,128,128]{4,3,2,1,0:T(8,128)} async-done(((f32[4,1,4,128,128]{4,3,2,1,0:T(8,128)}), f32[4,1,4,128,128]{4,3,2,1,0:T(8,128)}) %all-reduce.3.cloned.1.call-update) | async-done | bytes 1048592
  306.1 1.9 constant_dynamic-slice_fusion.2
  (50 shorter events, 0.7 us)
Async XLA Ops:
  6.5 1.0 copy-start
  6.5 30.1 %copy-start.2 = (s32[1,1,7]{2,1,0:T(1,128)S(1)}, s32[1,1,7]{2,1,0:T(1,128)}, u32[]{:S(2)}) copy-start(s32[1,1,7]{2,1,0:T(1,128)} %param.8) | copy-start | bytes 88
  6.5 44.6 %copy-start.1 = (s32[16,1,7]{0,1,2:T(1,128)S(1)}, s32[16,1,7]{0,1,2:T(1,128)}, u32[]{:S(2)}) copy-start(s32[16,1,7]{0,1,2:T(1,128)} %param.10) | copy-start | bytes 1348
  6.5 183.3 %all-gather.2.cloned.1.call-start = ((), (), s32[]{:S(2)}) async-start(), calls=%async_computation | async-start | bytes 36700160 | tf_op jit(solution)/shard_map/all_gather | solution.py:32
  7.3 298.8 %all-reduce.3.cloned.1.call-start = ((), (), s32[]{:S(2)}) async-start(), calls=%async_computation.1 | async-start | bytes 2097152
  7.6 15.6 %collective-permute-start = (f32[1,1,7,128,128]{4,3,2,1,0:T(8,128)S(1)}, f32[1,1,7,128,128]{4,3,2,1,0:T(8,128)S(1)}, u32[]{:S(2)}, u32[]{:S(2)}) collective-permute-start(f32[1,1,7,128,128]{4,3,2,1,0:T(8,128)S(1)} %copy-done), channel_id=1, source_target_pairs={{0,2},{2,4},{4,6},{6,0},{1,3},{3,5},{5,7},{7,1},{8,10},{10,12},{12... | collective-permute-start | bytes 1376264 | tf_op jit(solution)/shard_map/ppermute | solution.py:40
  23.1 13.5 %collective-permute-start.1 = (f32[1,1,7,128,128]{4,3,2,1,0:T(8,128)S(1)}, f32[1,1,7,128,128]{4,3,2,1,0:T(8,128)S(1)}, u32[]{:S(2)}, u32[]{:S(2)}) collective-permute-start(f32[1,1,7,128,128]{4,3,2,1,0:T(8,128)S(1)} %collective-permute-done), channel_id=1, source_target_pairs={{0,2},{2,4},{4,6},{6,0},{1,3},{3,5},{5,7},{7,1},{8,10},{10,12},{12... | collective-permute-start | bytes 1376264 | tf_op jit(solution)/shard_map/ppermute | solution.py:40
  36.6 20.0 %collective-permute-start.2 = (f32[1,1,7,128,128]{4,3,2,1,0:T(8,128)S(1)}, f32[1,1,7,128,128]{4,3,2,1,0:T(8,128)S(1)}, u32[]{:S(2)}, u32[]{:S(2)}) collective-permute-start(f32[1,1,7,128,128]{4,3,2,1,0:T(8,128)S(1)} %collective-permute-done.1), channel_id=1, source_target_pairs={{0,2},{2,4},{4,6},{6,0},{1,3},{3,5},{5,7},{7,1},{8,10},{10,12},{12... | collective-permute-start | bytes 1376264 | tf_op jit(solution)/shard_map/ppermute | solution.py:40
  56.8 133.0 %copy-start.3 = (s32[4,1,4]{2,1,0:T(1,128)S(1)}, s32[4,1,4]{2,1,0:T(1,128)}, u32[]{:S(2)}) copy-start(s32[4,1,4]{2,1,0:T(1,128)} %param.11) | copy-start | bytes 196
  189.8 76.0 %copy-start.4 = (u32[32]{0:T(128)S(1)}, u32[32]{0:T(128)}, u32[]{:S(2)}) copy-start(u32[32]{0:T(128)} %constant.195) | copy-start | bytes 388
Sparse Core Ops, SparseCore 0:
  8.9 180.8 all-gather.1
  266.0 40.0 all-reduce.2
